TPU v7x, 32 devices: a whole 2x2x4 slice. The times are simulated.
32 devices in a mesh: wave: 16 (over z, x, core), level: 2 (over y).
Axes of the slice: x: 2, y: 2, z: 4, core: 2. Of those that a mesh axis runs over, the one named last changes fastest.
Arguments:
- state: float32 [4, 64, 256, 2, 256], P(None, 'level', 'wave'), may hold values from -0.02 to 0.02
- legendre: float32 [256, 384, 256], P('wave'), may hold values from -6 to 6
- lat_weight: float32 [384], P('wave'), may hold values from 0.8 to 2
- modes: float32 [64, 64], replicated, may hold values from -1 to 1, as said below
- mode_rates: float32 [64], replicated, may hold values from 1e-05 to 0.003
- diffusion: float32 [4], replicated, may hold values from 0.3 to 3
- norm_gain: float32 [256], replicated, may hold values from 0.5 to 1.5
- w_first: bfloat16 [1024, 256], replicated, may hold values from -0.375 to 0.375
- b_first: float32 [1024], replicated, may hold values from -3 to 3
- w_second: bfloat16 [1024, 1024], replicated, may hold values from -0.1875 to 0.1875
- b_second: float32 [1024], replicated, may hold values from -3 to 3
- w_third: bfloat16 [256, 1024], replicated, may hold values from -0.1875 to 0.1875
- b_third: float32 [256], replicated, may hold values from -1.2 to 1.2
Outputs:
- next_state: float32 [4, 64, 256, 2, 256], P(None, 'level', 'wave')
Inputs may be any that keep to these rules, and one draw needn't show every extreme that they name: `modes`: orthogonal: its transpose is its inverse.
All inputs are finite; a program needn't handle non-finite values.
Results may differ from a plain program's by a relative error of at most 0.0011.
Values may be sent and summed in bfloat16 or wider, within the bound.
A program may use at most 192 MiB of HBM per device.

v0:
```python
import functools

import jax
import jax.numpy as jnp
from jax import lax
from jax.experimental import pallas as pl
from jax.experimental.pallas import tpu as pltpu
from jax.sharding import PartitionSpec as P

high = lax.Precision.HIGH
norm_eps = 1e-06
axes = ("wave", "level")
send_scale = 1024.0


def phase_angles(waves, longitudes):
    wave_idx = jnp.arange(waves, dtype=jnp.int32)
    lon_idx = jnp.arange(longitudes, dtype=jnp.int32)
    phase_turns = wave_idx[:, None] * lon_idx[None, :] % longitudes
    return (2.0 * jnp.pi / longitudes * phase_turns.astype(jnp.float32), wave_idx)


def synthesis_table(waves, longitudes):
    angle_table, wave_idx = phase_angles(waves, longitudes)
    factor = jnp.where(wave_idx == 0, 1.0, 2.0).astype(jnp.float32)[:, None]
    return jnp.stack([factor * jnp.cos(angle_table), -factor * jnp.sin(angle_table)], axis=1)


def analysis_table(waves, longitudes):
    angle_table, _ = phase_angles(waves, longitudes)
    return jnp.stack([jnp.cos(angle_table), -jnp.sin(angle_table)], axis=1) / longitudes


def contract_last(left, right):
    return lax.dot_general(
        left, right, (((1,), (1,)), ((), ())), preferred_element_type=jnp.float32
    )


def physics_kernel(grid_ref, lat_ref, gain_ref, w1_ref, b1_ref, w2_ref, b2_ref, w3_ref, b3_ref, out_ref, top_ref):
    grid_rows = grid_ref[0]
    values = grid_rows.astype(jnp.bfloat16).astype(jnp.float32)
    inverse_rms = lax.rsqrt(jnp.mean(values * values, axis=1, keepdims=True) + norm_eps)
    normed = (values * inverse_rms * gain_ref[...]).astype(jnp.bfloat16)
    hidden = jax.nn.gelu(contract_last(normed, w1_ref[...]) + b1_ref[...]).astype(jnp.bfloat16)
    hidden = jax.nn.gelu(contract_last(hidden, w2_ref[...]) + b2_ref[...]).astype(jnp.bfloat16)
    tendency = (contract_last(hidden, w3_ref[...]) + b3_ref[...]).astype(jnp.bfloat16)
    updated = (grid_rows + tendency.astype(jnp.float32)) * lat_ref[pl.program_id(0)]
    out_ref[0] = updated
    top_ref[0] = jnp.max(jnp.abs(updated), axis=0, keepdims=True)


def column_step(grid, lat, gain, w1, b1, w2, b2, w3, b3):
    rows, lon, feats = grid.shape
    hid = w1.shape[0]
    whole = lambda *shape: pl.BlockSpec(shape, lambda i: (0,) * len(shape))
    block = pl.BlockSpec((1, lon, feats), lambda i: (i, 0, 0))
    return pl.pallas_call(
        physics_kernel,
        grid=(rows,),
        out_shape=(
            jax.ShapeDtypeStruct((rows, lon, feats), jnp.float32),
            jax.ShapeDtypeStruct((rows, 1, feats), jnp.float32),
        ),
        in_specs=[
            block,
            pl.BlockSpec(memory_space=pltpu.SMEM),
            whole(1, feats),
            whole(hid, feats),
            whole(1, hid),
            whole(hid, hid),
            whole(1, hid),
            whole(feats, hid),
            whole(1, feats),
        ],
        out_specs=(block, pl.BlockSpec((1, 1, feats), lambda i: (i, 0, 0))),
        compiler_params=pltpu.CompilerParams(vmem_limit_bytes=56 * 1024 * 1024),
    )(grid, lat, gain[None], w1, b1[None], w2, b2[None], w3, b3[None])


def body(
    longitudes,
    state,
    legendre,
    lat_weight,
    modes,
    mode_rates,
    diffusion,
    norm_gain,
    w_first,
    b_first,
    w_second,
    b_second,
    w_third,
    b_third,
):
    fields, lev_dev, m_dev, parts, degrees = state.shape
    levels = modes.shape[0]
    waves = degrees
    wave_count = lax.axis_size("wave")
    level_count = lax.axis_size("level")
    lat_band = lat_weight.shape[0]
    lat_own = -(-lat_band // level_count)
    lat_extra = lat_own * level_count - lat_band
    wave_global = lax.axis_index("wave") * m_dev + jnp.arange(m_dev, dtype=jnp.int32)
    degree_index = wave_global[:, None] + jnp.arange(degrees, dtype=jnp.int32)[None, :]
    kept_mask = (degree_index < waves).astype(jnp.float32)
    basis = legendre * kept_mask[:, None, :]
    if lat_extra:
        basis = basis.reshape(m_dev, wave_count, lat_band, degrees)
        basis = jnp.pad(basis, ((0, 0), (0, 0), (0, lat_extra), (0, 0)))
        basis = basis.reshape(m_dev, -1, degrees)
        lat_weight = jnp.pad(lat_weight, (0, lat_extra))
    inverse_tab = synthesis_table(waves, longitudes).reshape(wave_count, m_dev, parts, longitudes)
    forward_tab = analysis_table(waves, longitudes).reshape(wave_count, m_dev, parts, longitudes)

    band = jnp.einsum("flmcj,maj->amcfl", state, basis, precision=high)
    band = (band * send_scale).astype(jnp.float16)
    band = band.reshape(wave_count * level_count, lat_own, m_dev, parts, fields, lev_dev)
    band = lax.all_to_all(band, axes, split_axis=0, concat_axis=0, tiled=True)
    band = band.reshape(wave_count, level_count, lat_own, m_dev, parts, fields, lev_dev)
    band = band.astype(jnp.float32) * (1.0 / send_scale)
    grid = jnp.einsum("wvamcfl,wmco->aovfl", band, inverse_tab, precision=high)
    feats = fields * levels
    grid = grid.reshape(lat_own, longitudes, feats)

    def slabs_first(x):
        split = x.reshape((fields, level_count, lev_dev) + x.shape[1:])
        return jnp.swapaxes(split, 0, 1).reshape(x.shape)

    lat = lax.dynamic_slice_in_dim(lat_weight, lax.axis_index("level") * lat_own, lat_own, 0)
    updated, tops = column_step(
        grid,
        lat,
        slabs_first(norm_gain),
        slabs_first(w_first.T).T,
        b_first,
        w_second,
        b_second,
        slabs_first(w_third),
        slabs_first(b_third),
    )
    top = jnp.maximum(jnp.max(tops), 1e-25)
    reach = 32768.0 / levels**0.5
    tops_all = lax.all_gather(top / reach, axes).reshape(wave_count, level_count)

    wave = jnp.einsum("aok,wmco->wmcak", updated, forward_tab, precision=high)
    wave = wave * (reach / top)
    wave = wave.reshape(wave_count, m_dev, parts, lat_own, level_count, fields, lev_dev)
    modal = jnp.einsum(
        "wmcavl,vlk->wmcak",
        wave[..., 1, :],
        modes.reshape(level_count, lev_dev, levels),
        precision=high,
    )
    others = jnp.concatenate([wave[..., :1, :], wave[..., 2:, :]], axis=-2)
    others = others.reshape(wave_count, m_dev, parts, lat_own, level_count, (fields - 1) * lev_dev)
    others = jnp.moveaxis(others, 4, 1)
    modal = jnp.broadcast_to(modal[:, None], others.shape[:-1] + (levels,))
    sent = jnp.concatenate([others, modal], axis=-1).astype(jnp.float16)
    sent = sent.reshape((wave_count * level_count,) + sent.shape[2:])
    got = lax.all_to_all(sent, axes, split_axis=0, concat_axis=0, tiled=True)
    got = got.reshape((wave_count, level_count) + got.shape[1:]).astype(jnp.float32)
    got = got * tops_all[:, :, None, None, None, None]
    basis_split = basis.reshape(m_dev, wave_count, level_count, lat_own, degrees)
    spectral = jnp.einsum("wvmcaq,mwvaj->qmcj", got, basis_split, precision=high)

    growth = (degree_index * (degree_index + 1)).astype(jnp.float32)
    plain = spectral[: (fields - 1) * lev_dev].reshape(fields - 1, lev_dev, m_dev, parts, degrees)
    divisor = 1.0 + mode_rates[:, None, None, None] * growth[None, :, None, :]
    amplitude = spectral[(fields - 1) * lev_dev :] / divisor
    own_rows = lax.dynamic_slice_in_dim(modes, lax.axis_index("level") * lev_dev, lev_dev, 0)
    solved = jnp.einsum("lk,kmcj->lmcj", own_rows, amplitude, precision=high)
    combined = jnp.concatenate([plain[:1], solved[None], plain[1:]], axis=0)
    scaled_growth = growth / (waves * (waves - 1))
    damping = 1.0 + diffusion[:, None, None] * (scaled_growth * scaled_growth)[None]
    return combined / damping[:, None, :, None, :]


def solution(mesh):
    def step(state, legendre, *rest):
        longitudes = 2 * legendre.shape[1]
        mapped = jax.shard_map(
            functools.partial(body, longitudes),
            mesh=mesh,
            in_specs=(P(None, "level", "wave", None, None), P("wave", None, None), P("wave")) + (P(),) * 10,
            out_specs=P(None, "level", "wave", None, None),
            check_vma=False,
        )
        return mapped(state, legendre, *rest)

    return step
```

profile of v0, /device:TPU:0, one launch (start us, length us, event | category | flops | bytes accessed | tf_op | source)
XLA Modules:
  0.0 613.5 jit_solution(5170881032946603043)
XLA Ops:
  0.0 0.0 copy-start
  0.0 0.1 fusion.46
  0.1 6.6 %fusion.51 = f32[16,384,256,1,1]{2,0,1,4,3:T(8,128)S(1)} fusion(f32[16,256]{1,0:T(8,128)S(1)} %fusion.46, f32[16,384,256]{2,1,0:T(8,128)} %param.14), kind=kLoop, calls=%fused_computation.64 | loop fusion | flops 1572864 | bytes 12599296 | tf_op jit(solution)/shard_map/mul | solution.py:108
  6.7 0.0 copy-done.2
  6.7 8.9 %fusion.14 = f16[384,16,2,4,32]{0,4,2,3,1:T(8,128)(2,1)S(1)} fusion(f32[4,32,16,2,256]{4,3,2,1,0:T(2,128)S(1)} %copy-done.2, f32[16,384,256,1,1]{2,0,1,4,3:T(8,128)S(1)} %fusion.51), kind=kOutput, calls=%fused_computation.21 | convolution fusion | flops 2419064832 | bytes 13631488 | tf_op jit(solution)/shard_map/flmcj,maj->amcfl/dot_general | solution.py:117
  15.6 21.9 %copy.29 = f16[384,16,2,4,32]{4,1,3,2,0:T(8,128)(2,1)} copy(f16[384,16,2,4,32]{0,4,2,3,1:T(8,128)(2,1)S(1)} %fusion.14) | data formatting | bytes 6291456 | tf_op jit(solution)/shard_map/convert_element_type | solution.py:118
  37.4 17.7 %reshape.288 = f16[32,2,24576]{2,1,0:T(2,128)(2,1)} reshape(f16[32,12,2,4,16,32]{5,4,3,2,1,0:T(8,128)(2,1)} %bitcast.91) | data formatting | bytes 6291456
  55.2 7.6 %all-to-all-start = ((f16[32,2,24576]{2,1,0:T(2,128)(2,1)}), f16[32,2,24576]{2,1,0:T(2,128)(2,1)S(1)}, u32[]{:S(2)}, u32[]{:S(2)}) async-start(f16[32,2,24576]{2,1,0:T(2,128)(2,1)} %reshape.288), calls=%async_computation | async-start | bytes 6291456 | tf_op jit(solution)/shard_map/all_to_all | solution.py:120
  62.8 0.0 copy-done.8
  62.8 0.1 reshape.266
  62.9 0.7 broadcast_in_dim_reshape.7.gain_ref
  63.6 2.0 copy.33
  65.6 1.9 copy.34
  67.5 2.1 copy.35
  69.5 1.9 copy.36
  71.4 0.0 copy-done.9
  71.4 0.1 reshape.271
  71.5 0.7 broadcast_in_dim_reshape.8.b3_ref
  72.2 0.0 copy-done.12
  72.2 0.6 dynamic_slice.6.lat_ref
  72.8 4.4 fusion.38
  77.2 1.3 fusion.27
  78.5 55.5 %all-to-all-done = f16[32,2,24576]{2,1,0:T(2,128)(2,1)S(1)} async-done(((f16[32,2,24576]{2,1,0:T(2,128)(2,1)}), f16[32,2,24576]{2,1,0:T(2,128)(2,1)S(1)}, u32[]{:S(2)}, u32[]{:S(2)}) %all-to-all-start) | async-done | bytes 3145760 | tf_op jit(solution)/shard_map/all_to_all | solution.py:120
  134.0 11.9 %reshape.289 = f16[32,12,2,4,16,32]{5,4,3,2,1,0:T(8,128)(2,1)} reshape(f16[32,2,24576]{2,1,0:T(2,128)(2,1)S(1)} %all-to-all-done) | data formatting | bytes 6291456
  145.9 14.7 %convert_multiply_fusion = f32[32,12,16,2,4,32]{5,2,4,3,1,0:T(8,128)} fusion(f16[32,12,2,4,16,32]{5,4,3,2,1,0:T(8,128)(2,1)} %reshape.289), kind=kLoop, calls=%fused_computation.3 | loop fusion | flops 3145728 | bytes 9437184 | tf_op jit(solution)/shard_map/mul | solution.py:122
  160.6 0.0 copy-done.6
  160.6 51.2 %fusion.11 = f32[12,768,2,4,32]{1,4,3,0,2:T(8,128)} fusion(f32[16,2,12,16,2,4,32]{6,3,5,4,2,1,0:T(8,128)} %bitcast.93, f32[16,16,1,768]{3,0,1,2:T(8,128)S(1)} %copy-done.6, f32[16,16,1,768]{3,0,1,2:T(8,128)S(1)} %copy-done.7), kind=kOutput, calls=%fused_computation.20 | convolution fusion | flops 7248150528 | bytes 17301504 | tf_op jit(solution)/shard_map/wvamcfl,wmco->aovfl/dot_general | solution.py:123
  211.8 8.5 %copy.31 = f32[12,768,2,4,32]{1,4,3,2,0:T(8,128)} copy(f32[12,768,2,4,32]{1,4,3,0,2:T(8,128)} %fusion.11) | data formatting | bytes 18874368 | tf_op jit(solution)/shard_map/wvamcfl,wmco->aovfl/transpose | solution.py:123
  220.3 9.6 %copy.38.grid_ref = f32[12,768,256]{2,1,0:T(8,128)} copy(f32[12,768,256]{1,2,0:T(8,128)} %bitcast.92) | data formatting | bytes 18874368 | tf_op jit(solution)/shard_map/reshape | solution.py:125
  229.9 43.4 %shard_map.127 = (f32[12,768,256]{2,1,0:T(8,128)}, f32[12,1,256]{2,1,0:T(1,128)}) custom-call(f32[12,768,256]{2,1,0:T(8,128)} %copy.38.grid_ref, f32[12]{0:T(128)} %dynamic_slice.6.lat_ref, f32[1,256]{1,0:T(1,128)} %broadcast_in_dim_reshape.7.gain_ref, bf16[1024,256]{1,0:T(8,128)(2,1)} %bitcast.99, f32[1,1024]{1,0:T(1,128)} %bitcast.106, ...), custom_call_target="tpu_custom_call" | custom-call | tf_op jit(solution)/shard_map/pallas_call | solution.py:58
  273.3 1.4 reduce_max.9
  275.4 13.4 %broadcast_multiply_fusion = f32[16,16,2,12,256]{4,1,3,2,0:T(8,128)} fusion(f32[]{:T(128)S(6)} %div.36, f32[12,768,256]{2,1,0:T(8,128)} %get-tuple-element.7, f32[16,16,2,768,1]{3,0,1,2,4:T(8,128)S(1)} %copy-done.4), kind=kOutput, calls=%fused_computation.23 | convolution fusion | flops 7249330176 | bytes 17301508 | tf_op jit(solution)/shard_map/aok,wmco->wmcak/dot_general | solution.py:147
  288.8 18.4 %reshape.272 = f32[16,16,2,12,2,4,32]{6,5,4,1,3,2,0:T(4,128)} reshape(f32[16,16,2,12,256]{4,1,3,2,0:T(8,128)} %broadcast_multiply_fusion) | data formatting | bytes 12582912 | tf_op jit(solution)/shard_map/reshape | solution.py:149
  307.2 12.5 %slice.39 = f32[16,16,2,12,2,1,32]{6,5,4,1,3,2,0:T(1,128)} slice(f32[16,16,2,12,2,4,32]{6,5,4,1,3,2,0:T(4,128)} %reshape.272), slice={[0:16], [0:16], [0:2], [0:12], [0:2], [1:2], [0:32]} | slice | bytes 3145728 | tf_op jit(solution)/shard_map/slice | solution.py:152
  319.7 10.6 %copy_convert_fusion = f16[16,16,2,12,2,4,32]{6,5,1,4,3,2,0:T(4,128)(2,1)S(1)} fusion(f32[16,16,2,12,2,4,32]{6,5,4,1,3,2,0:T(4,128)} %reshape.272), kind=kLoop, calls=%fused_computation | loop fusion | flops 1572864 | bytes 9437184 | tf_op jit(solution)/shard_map/convert.10 | solution.py:190
  330.4 8.4 %slice.38 = f16[16,16,2,12,2,2,32]{6,5,1,4,3,2,0:T(2,128)(2,1)S(1)} slice(f16[16,16,2,12,2,4,32]{6,5,1,4,3,2,0:T(4,128)(2,1)S(1)} %copy_convert_fusion), slice={[0:16], [0:16], [0:2], [0:12], [0:2], [2:4], [0:32]} | slice | bytes 3145728 | tf_op jit(solution)/shard_map/slice | solution.py:156
  338.8 7.2 %slice.37 = f16[16,16,2,12,2,1,32]{6,5,1,4,3,2,0:T(2,128)(2,1)S(1)} slice(f16[16,16,2,12,2,4,32]{6,5,1,4,3,2,0:T(4,128)(2,1)S(1)} %copy_convert_fusion), slice={[0:16], [0:16], [0:2], [0:12], [0:2], [0:1], [0:32]} | slice | bytes 1572864 | tf_op jit(solution)/shard_map/slice | solution.py:156
  346.0 20.7 %pad_maximum_fusion = f16[16,16,2,12,2,3,32]{6,5,1,4,3,2,0:T(4,128)(2,1)} fusion(f16[16,16,2,12,2,2,32]{6,5,1,4,3,2,0:T(2,128)(2,1)S(1)} %slice.38, f16[16,16,2,12,2,1,32]{6,5,1,4,3,2,0:T(2,128)(2,1)S(1)} %slice.37), kind=kLoop, calls=%fused_computation.4 | loop fusion | flops 1179648 | bytes 4718592 | tf_op jit(solution)/shard_map/concatenate | solution.py:156
  366.8 20.1 %reshape.273 = f16[16,16,2,12,2,96]{5,1,4,3,2,0:T(8,128)(2,1)S(1)} reshape(f16[16,16,2,12,2,3,32]{6,5,1,4,3,2,0:T(4,128)(2,1)} %pad_maximum_fusion) | data formatting | bytes 4718592 | tf_op jit(solution)/shard_map/reshape | solution.py:157
  386.9 0.9 copy.41
  387.8 0.0 copy-done
  387.8 5.4 bitcast_convert_fusion
  393.2 0.8 broadcast_in_dim.20
  394.0 6.2 %pad_maximum_fusion.1 = f16[32,16,2,12,160]{4,1,3,2,0:T(8,128)(2,1)} fusion(f16[32,16,2,12,64]{4,1,3,2,0:T(8,128)(2,1)S(1)} %bitcast.97, f16[32,16,2,12,96]{4,1,3,2,0:T(8,128)(2,1)S(1)} %bitcast.96), kind=kLoop, calls=%fused_computation.10 | loop fusion | flops 1966080 | bytes 7864320 | tf_op jit(solution)/shard_map/concatenate | solution.py:160
  400.2 3.7 all-to-all-start.1
  404.0 0.1 fusion.42
  404.0 0.1 multiply_multiply_fusion
  404.1 0.1 multiply_add_fusion.1
  404.2 0.0 copy-done.11
  404.2 1.1 multiply_add_fusion
  405.3 9.1 %copy_multiply_fusion = f32[16,384,256]{2,0,1:T(8,128)} fusion(f32[16,384,256]{2,1,0:T(8,128)} %param.14, f32[16,256]{1,0:T(8,128)S(1)} %fusion.46), kind=kLoop, calls=%fused_computation.16 | loop fusion | flops 1572864 | bytes 12599296 | tf_op jit(solution)/shard_map/mul | solution.py:108
  414.4 0.1 dynamic-update-slice
  414.5 150.0 %all-reduce = f32[32]{0:T(128)S(1)} all-reduce(f32[32]{0:T(128)S(1)} %dynamic-update-slice), channel_id=1, replica_groups=mesh['wave'=16,'level'=2] {'wave','level'}, use_global_device_ids=true, to_apply=%add | all-reduce | flops 32 | bytes 256
  564.5 0.1 mul.288
  564.6 0.0 all-to-all-done.1
  564.6 9.4 %convert_multiply_fusion.1 = f32[16,2,16,2,12,160]{5,2,4,3,1,0:T(8,128)} fusion(f16[16,2,16,2,12,160]{5,2,4,3,1,0:T(8,128)(2,1)} %bitcast.58, f32[16,2]{1,0:T(8,128)S(1)} %mul.288), kind=kLoop, calls=%fused_computation.5 | loop fusion | flops 3932160 | bytes 11796608 | tf_op jit(solution)/shard_map/mul | solution.py:164
  574.0 29.3 %fusion.17 = f32[160,16,2,256]{3,0,2,1:T(8,128)} fusion(f32[16,2,16,2,12,160]{5,2,4,3,1,0:T(8,128)} %convert_multiply_fusion.1, f32[16,16,2,12,256,1]{4,0,3,2,1,5:T(8,128)S(1)} %bitcast.94), kind=kOutput, calls=%fused_computation.24 | convolution fusion | flops 3019898880 | bytes 19398656 | tf_op jit(solution)/shard_map/wvmcaq,mwvaj->qmcj/dot_general | solution.py:166
  603.3 1.5 slice_bitcast_fusion
  604.8 0.4 slice-done
  605.2 1.9 copy.47
  607.1 0.7 fusion.31
  607.8 0.8 copy.46
  608.6 0.8 copy.45
  609.4 3.6 maximum_divide_fusion
  (25 shorter events, 0.1 us)
Async XLA Ops:
  0.0 387.8 %copy-start = (f32[64,64]{1,0:T(8,128)S(1)}, f32[64,64]{1,0:T(8,128)}, u32[]{:S(2)}) copy-start(f32[64,64]{1,0:T(8,128)} %param.16) | copy-start | bytes 49156
  0.1 6.6 %copy-start.2 = (f32[4,32,16,2,256]{4,3,2,1,0:T(2,128)S(1)}, f32[4,32,16,2,256]{4,3,2,1,0:T(2,128)}, u32[]{:S(2)}) copy-start(f32[4,32,16,2,256]{4,3,2,1,0:T(2,128)} %param.13) | copy-start | bytes 12582916
  55.2 7.6 %copy-start.8 = (f32[256]{0:T(256)S(1)}, f32[256]{0:T(256)}, u32[]{:S(2)}) copy-start(f32[256]{0:T(256)} %param.19) | copy-start | bytes 3076
  55.2 16.2 %copy-start.9 = (f32[256]{0:T(256)S(1)}, f32[256]{0:T(256)}, u32[]{:S(2)}) copy-start(f32[256]{0:T(256)} %param.25) | copy-start | bytes 3076
  55.2 17.0 %copy-start.12 = (f32[24]{0:T(128)S(1)}, f32[24]{0:T(128)}, u32[]{:S(2)}) copy-start(f32[24]{0:T(128)} %param.15) | copy-start | bytes 292
  55.2 78.8 %all-to-all-start = ((f16[32,2,24576]{2,1,0:T(2,128)(2,1)}), f16[32,2,24576]{2,1,0:T(2,128)(2,1)S(1)}, u32[]{:S(2)}, u32[]{:S(2)}) async-start(f16[32,2,24576]{2,1,0:T(2,128)(2,1)} %reshape.288), calls=%async_computation | async-start | bytes 6291456 | tf_op jit(solution)/shard_map/all_to_all | solution.py:120
  145.9 14.7 %copy-start.6 = (f32[16,16,1,768]{3,0,1,2:T(8,128)S(1)}, f32[16,16,1,768]{3,0,1,2:T(8,128)}, u32[]{:S(2)}) copy-start(f32[16,16,1,768]{3,0,1,2:T(8,128)} %get-tuple-element.10) | copy-start | bytes 2359300
  145.9 14.7 %copy-start.7 = (f32[16,16,1,768]{3,0,1,2:T(8,128)S(1)}, f32[16,16,1,768]{3,0,1,2:T(8,128)}, u32[]{:S(2)}) copy-start(f32[16,16,1,768]{3,0,1,2:T(8,128)} %get-tuple-element.12) | copy-start | bytes 2359300
  229.9 45.5 %copy-start.4 = (f32[16,16,2,768,1]{3,0,1,2,4:T(8,128)S(1)}, f32[16,16,2,768,1]{3,0,1,2,4:T(8,128)}, u32[]{:S(2)}) copy-start(f32[16,16,2,768,1]{3,0,1,2,4:T(8,128)} %fusion.27) | copy-start | bytes 4718596
  400.2 3.9 copy-start.10
  400.2 4.0 copy-start.11
  400.2 164.4 %all-to-all-start.1 = ((f16[32,16,2,12,160]{4,1,3,2,0:T(8,128)(2,1)}), f16[32,16,2,12,160]{4,1,3,2,0:T(8,128)(2,1)}, u32[]{:S(2)}, u32[]{:S(2)}) async-start(f16[32,16,2,12,160]{4,1,3,2,0:T(8,128)(2,1)} %pad_maximum_fusion.1), calls=%async_computation.1 | async-start | bytes 12582912 | tf_op jit(solution)/shard_map/all_to_all | solution.py:162
  564.6 9.4 %copy-start.1 = (f32[16,384,256]{2,0,1:T(8,128)S(1)}, f32[16,384,256]{2,0,1:T(8,128)}, u32[]{:S(2)}) copy-start(f32[16,384,256]{2,0,1:T(8,128)} %copy_multiply_fusion) | copy-start | bytes 18874372
  603.3 1.9 slice-start
  603.3 3.8 copy-start.3
  603.3 3.8 copy-start.5
where the time goes:
time: 623 us; the launch traced here: 613 us
  local copies, waits for them, and re-layouts  154 us (25%)
  blocking collectives  150 us (24%)
  matrix products  109 us (17%)
  other arithmetic  89.5 us (14%)
  waiting for transfers between devices  55.5 us (9%)
  Pallas kernels  43.4 us (7%)
  starting transfers between devices  11.3 us (2%)
    unnamed x1, blocking collectives  150 us
    all_to_all x1, waiting for transfers between devices, body(): band = lax.all_to_all(band, axes, split_axis=0, concat_axis=0, tiled=True)  55.5 us
    dot_general x1, matrix products, body(): grid = jnp.einsum('wvamcfl,wmco->aovfl', band, inverse_tab, precision=high)  51.2 us
    pallas_call x1, Pallas kernels, column_step(): pl.pallas_call(physics_kernel, grid=(rows,), out_shape=(jax.ShapeDtypeStr...  43.4 us
    unnamed x31, local copies, waits for them, and re-layouts  31.8 us
    dot_general x1, matrix products, body(): jnp.einsum('wvmcaq,mwvaj->qmcj', got, basis_split, precision=high)  29.3 us
    convert_element_type x1, local copies, waits for them, and re-layouts, body(): band = (band * send_scale).astype(jnp.float16)  21.9 us
    concatenate x1, other arithmetic, body(): others = jnp.concatenate([wave[..., :1, :], wave[..., 2:, :]], axis=-2)  20.7 us
  transfers between devices with their start and end apart: 2, of which 1 were waited for; matrix products, arithmetic and copies ran while one was open for 4% of the time, Pallas kernels for 0%

commit v1 on v0

--- a/solution.py
+++ b/solution.py
@@ -1,7 +1,9 @@
 import functools
+import math
 
 import jax
 import jax.numpy as jnp
+import numpy as np
 from jax import lax
 from jax.experimental import pallas as pl
 from jax.experimental.pallas import tpu as pltpu
@@ -78,7 +80,7 @@
     )(grid, lat, gain[None], w1, b1[None], w2, b2[None], w3, b3[None])
 
 
-def body(
+def general_body(
     longitudes,
     state,
     legendre,
@@ -177,11 +179,454 @@
     return combined / damping[:, None, :, None, :]
 
 
+chunks = 3
+vmem_limit = 60 * 1024 * 1024
+
+
+def split_table(table):
+    high_part = np.asarray(table, jnp.bfloat16)
+    low_part = np.asarray(table - high_part.astype(np.float64), jnp.bfloat16)
+    return np.stack([high_part, low_part])
+
+
+def fourier_tables(waves, longitudes, wave_count, scale):
+    half = longitudes // 2
+    per_wave = waves // wave_count
+    synthesis, analysis = [], []
+    for parity in range(2):
+        order = np.arange(waves).reshape(wave_count, per_wave // 2, 2)[:, :, parity]
+        turns = order[:, :, None] * np.arange(half)[None, None, :] % longitudes
+        angles = 2.0 * np.pi / longitudes * turns
+        pair = np.stack([np.cos(angles), -np.sin(angles)], axis=1)
+        factor = np.where(order == 0, 1.0, 2.0)[:, None, :, None]
+        synthesis.append(split_table((pair * factor / scale).reshape(-1, half).T))
+        analysis.append(split_table((pair / longitudes).reshape(-1, half)))
+    return np.stack(synthesis), np.stack(analysis)
+
+
+def halves(x):
+    top = x.astype(jnp.bfloat16)
+    return top, (x - top.astype(jnp.float32)).astype(jnp.bfloat16)
+
+
+def dot3(left, right, dims):
+    dot = lambda a, b: lax.dot_general(a, b, (dims, ((), ())), preferred_element_type=jnp.float32)
+    return dot(left[0], right[0]) + (dot(left[0], right[1]) + dot(left[1], right[0]))
+
+
+def kept(block, wave_index):
+    degree = lax.broadcasted_iota(jnp.int32, block.shape, 1)
+    return jnp.where(degree + wave_index < block.shape[1], block, 0.0)
+
+
+def row_of(m, part, m_dev):
+    half = m_dev // 2
+    return (m % 2) * m_dev + part * half + m // 2
+
+
+send_octaves, send_top = 32, 5
+back_octaves, back_top = 56, 24
+
+
+def encode(x, octaves, top):
+    floor_power = float(top - octaves)
+    magnitude = jnp.abs(x)
+    power = jnp.floor(jnp.log2(jnp.maximum(magnitude, 2.0**floor_power)))
+    ratio = 250.0 / (octaves + 1)
+    place = (magnitude * jnp.exp2(-power) + (power - floor_power)) * ratio
+    step = jnp.floor(place)
+    code = jnp.exp2(step - 125.0) * (place - step + 1.0)
+    return jnp.where(x < 0.0, -code, code).astype(jnp.bfloat16)
+
+
+def decode(code, octaves, top):
+    floor_power = float(top - octaves)
+    code = code.astype(jnp.float32)
+    magnitude = jnp.abs(code)
+    step = jnp.floor(jnp.log2(magnitude))
+    place = (magnitude * jnp.exp2(-step) + (step + 124.0)) * ((octaves + 1) / 250.0)
+    power = jnp.floor(place)
+    lead = jnp.minimum(power, 1.0)
+    value = (place - power + lead) * jnp.exp2(power - lead + floor_power)
+    return jnp.where(code < 0.0, -value, value)
+
+
+def own_place():
+    slabs = lax.axis_size("level")
+    count = lax.axis_size("wave") * slabs
+    return lax.axis_index("wave") * slabs + lax.axis_index("level"), count, slabs
+
+
+def start_wave(src, dst, sems, at):
+    me, count, slabs = own_place()
+    half = count // 2
+    side = me // half
+
+    def to(base, first):
+        peer = base * half + lax.rem(me + first, half)
+        pltpu.make_async_remote_copy(
+            src_ref=src.at[at, peer],
+            dst_ref=dst.at[at, me],
+            send_sem=sems.at[0, at],
+            recv_sem=sems.at[1, at],
+            device_id=(peer // slabs, lax.rem(peer, slabs)),
+            device_id_type=pl.DeviceIdType.MESH,
+        ).start()
+        return 0
+
+    lax.fori_loop(0, half, lambda k, _: to(1 - side, k), 0)
+    lax.fori_loop(1, half, lambda k, _: to(side, k), 0)
+
+
+def wait_most(src, dst, sem, at, count):
+    most = pl.ds(0, count - 1)
+    pltpu.make_async_copy(src.at[at, most], dst.at[at, most], sem).wait()
+
+
+def whole_block(x):
+    return pl.BlockSpec(x.shape, lambda *_: (0,) * x.ndim)
+
+
+def remote_params():
+    return pltpu.CompilerParams(vmem_limit_bytes=vmem_limit, has_side_effects=True)
+
+
+def twice_gelu(x):
+    inner = x * (0.7978845608028654 + 0.7978845608028654 * 0.044715 * (x * x))
+    return (x + x * jnp.tanh(inner)).astype(jnp.bfloat16)
+
+
+def step_kernel(
+    lat_ref, diff_ref, state_ref, leg_ref, modes_ref, rates_ref, gain_ref, b1_ref, b2_ref, b3_ref, perm_ref, syn_hbm, ana_hbm, w1_hbm, w2_hbm, w3_hbm,
+    out_ref, swap_ref,
+    band_ref, there_ref, here_ref, back_ref, home_ref, total_ref, hold_ref, modal_ref, gain_own, b3_own, syn_ref, ana_ref, w1_ref, w2_ref, w3_ref,
+    there_sems, back_sems, swap_sems, load_sems,
+):
+    fields, lev_dev, m_block, parts, degrees = state_ref.shape
+    rows = back_ref.shape[0]
+    step = pl.program_id(0)
+    first_steps = (pl.num_programs(0) - rows) // 2
+    blocks = first_steps // chunks
+    grid_steps = first_steps + rows
+    m_dev = blocks * m_block
+    feats = fields * lev_dev
+    mc = m_dev * parts
+    half = mc // 2
+    me, count, slabs = own_place()
+    waves = count // slabs
+    width = slabs * feats
+    per_chunk = rows // chunks
+    level = lax.axis_index("level")
+    loads = [
+        pltpu.make_async_copy(src, dst, load_sems.at[i])
+        for i, (src, dst) in enumerate(((syn_hbm, syn_ref), (ana_hbm, ana_ref), (w1_hbm, w1_ref), (w2_hbm, w2_ref), (w3_hbm, w3_ref)))
+    ]
+
+    @pl.when(step == 0)
+    def _():
+        for load in loads:
+            load.start()
+
+    @pl.when((step > 0) & (step <= first_steps) & (lax.rem(step, blocks) == 0))
+    def _():
+        start_wave(there_ref, here_ref, there_sems, step // blocks - 1)
+
+    @pl.when(step == blocks)
+    def _():
+        for load in loads:
+            load.wait()
+        order = [slice((f * slabs + v) * lev_dev, (f * slabs + v + 1) * lev_dev) for v in range(slabs) for f in range(fields)]
+        gain_own[...] = jnp.concatenate([gain_ref[:, at] for at in order], axis=1)
+        b3_own[...] = jnp.concatenate([b3_ref[:, at] for at in order], axis=1)
+        w3_ref[...] = jnp.concatenate([w3_ref[at, :] for at in order], axis=0) * 0.5
+        w1_ref[...] = jnp.dot(w1_ref[...], perm_ref[...], preferred_element_type=jnp.float32).astype(jnp.bfloat16)
+        w2_ref[...] = w2_ref[...] * 0.5
+        same = lax.broadcasted_iota(jnp.int32, (width, width), 0) == lax.broadcasted_iota(jnp.int32, (width, width), 1)
+        modal_ref[...] = same.astype(jnp.float32)
+        total_ref[...] = jnp.zeros_like(total_ref)
+        for v in range(slabs):
+            for k in range(slabs):
+                at = lambda i: slice(i * feats + lev_dev, i * feats + 2 * lev_dev)
+                modal_ref[at(v), at(k)] = modes_ref[v * lev_dev : (v + 1) * lev_dev, k * lev_dev : (k + 1) * lev_dev]
+
+    @pl.when(step < first_steps)
+    def _():
+        group, block = step // blocks, lax.rem(step, blocks)
+        for i in range(m_block):
+            m = block * m_block + i
+            basis = leg_ref[i].reshape(-1, degrees)
+            basis = halves(kept(basis, lax.axis_index("wave") * m_dev + m))
+            coeffs = [state_ref[:, :, i, c, :].reshape(feats, degrees) for c in range(parts)]
+            coeffs = halves(jnp.concatenate(coeffs, axis=0))
+            band = dot3(basis, coeffs, ((1,), (1,)))
+            for c in range(parts):
+                at = pl.ds(row_of(m, c, m_dev), band.shape[0], stride=mc)
+                band_ref[at, :] = band[:, c * feats : (c + 1) * feats]
+
+        @pl.when(block == blocks - 1)
+        def _():
+            size = per_chunk * mc
+            many = 4
+
+            def one(k, _):
+                part = band_ref[pl.ds(pl.multiple_of(k * many * size, 8), many * size), :]
+                there_ref[group, pl.ds(k * many, many)] = encode(part, send_octaves, send_top).reshape(many, size, feats)
+                return 0
+
+            lax.fori_loop(0, count // many, one, 0)
+            here_ref[group, me] = there_ref[group, me]
+
+    @pl.when((step > first_steps) & (step <= grid_steps))
+    def _():
+        start_wave(back_ref, home_ref, back_sems, step - first_steps - 1)
+
+    @pl.when((step >= first_steps) & (step < grid_steps))
+    def _():
+        row = step - first_steps
+        group, place = row // per_chunk, lax.rem(row, per_chunk)
+
+        @pl.when(place == 0)
+        def _():
+            wait_most(there_ref, here_ref, there_sems.at[1, group], group, count)
+
+        signs = []
+        for parity in range(2):
+            at = pl.ds(pl.multiple_of(place * mc + parity * half, half), half)
+            band = decode(here_ref[group, :, at, :], send_octaves, send_top).reshape(waves, slabs, half, feats)
+            band = [band[:, v].reshape(waves * half, feats) for v in range(slabs)]
+            band = halves(jnp.concatenate(band, axis=1))
+            signs.append(dot3((syn_ref[parity, 0], syn_ref[parity, 1]), band, ((1,), (0,))))
+        weight = lat_ref[group * (slabs * per_chunk) + level * per_chunk + place]
+        updated = []
+        for grid in (signs[0] + signs[1], signs[0] - signs[1]):
+            values = grid.astype(jnp.bfloat16).astype(jnp.float32)
+            inverse_rms = lax.rsqrt(jnp.mean(values * values, axis=1, keepdims=True) + norm_eps)
+            normed = (values * inverse_rms * gain_own[...]).astype(jnp.bfloat16)
+            hidden = twice_gelu(contract_last(normed, w1_ref[...]) + b1_ref[...])
+            hidden = twice_gelu(contract_last(hidden, w2_ref[...]) + b2_ref[...])
+            tendency = (contract_last(hidden, w3_ref[...]) + b3_own[...]).astype(jnp.bfloat16)
+            updated.append((grid + tendency.astype(jnp.float32)) * weight)
+        folded = (updated[0] + updated[1], updated[0] - updated[1])
+        modal = halves(modal_ref[...])
+        lane = lax.broadcasted_iota(jnp.int32, (waves, half // 2, feats), 2)
+        swapped = (lane >= lev_dev) & (lane < 2 * lev_dev)
+        for parity in range(2):
+            wave = dot3((ana_ref[parity, 0], ana_ref[parity, 1]), halves(folded[parity]), ((1,), (0,)))
+            wave = dot3(halves(wave), modal, ((1,), (0,)))
+            piece = lambda c, v: wave[:, v * feats : (v + 1) * feats].reshape(waves, 2, half // 2, feats)[:, c]
+            for v in range(slabs):
+                both = [jnp.where(swapped, piece(v, c), piece(c, v)) for c in range(2)]
+                both = encode(jnp.concatenate(both, axis=1), back_octaves, back_top)
+                for w in range(waves):
+                    back_ref[row, w * slabs + v, parity * half : (parity + 1) * half, :] = both[w]
+
+        home_ref[row, me] = back_ref[row, me]
+
+    late = step - grid_steps
+    late_group, late_block = late // blocks, lax.rem(late, blocks)
+
+    @pl.when((step >= grid_steps) & (late_block == 0))
+    def _():
+        wave_ref = band_ref.reshape(count, per_chunk, mc, feats)
+
+        def one(r, _):
+            row = late_group * per_chunk + r
+            wait_most(back_ref, home_ref, back_sems.at[1, row], row, count)
+            wave_ref[:, r] = decode(home_ref[row], back_octaves, back_top)
+            return 0
+
+        lax.fori_loop(0, per_chunk, one, 0)
+
+    def analysed(i):
+        m = late_block * m_block + i
+        basis = leg_ref[i].reshape(-1, degrees)
+        basis = halves(kept(basis, lax.axis_index("wave") * m_dev + m))
+        wave = [band_ref[pl.ds(row_of(m, c, m_dev), basis[0].shape[0], stride=mc), :] for c in range(parts)]
+        return m, dot3(halves(jnp.concatenate(wave, axis=1)), basis, ((0,), (0,)))
+
+    @pl.when((step >= grid_steps) & (late_group < chunks - 1))
+    def _():
+        for i in range(m_block):
+            m, part = analysed(i)
+            total_ref[m] = total_ref[m] + part
+
+    def swap(at):
+        return pltpu.make_async_remote_copy(
+            src_ref=hold_ref.at[at],
+            dst_ref=swap_ref.at[at],
+            send_sem=swap_sems.at[0, at],
+            recv_sem=swap_sems.at[1, at],
+            device_id=(lax.axis_index("wave"), 1 - level),
+            device_id_type=pl.DeviceIdType.MESH,
+        )
+
+    @pl.when((step >= grid_steps) & (late_group == chunks - 1))
+    def _():
+        @pl.when(late_block > 0)
+        def _():
+            swap(late_block - 1).start()
+
+        own = halves(modes_ref[pl.ds(pl.multiple_of(level * lev_dev, 8), lev_dev), :])
+        other = halves(modes_ref[pl.ds(pl.multiple_of((1 - level) * lev_dev, 8), lev_dev), :])
+        for i in range(m_block):
+            m, part = analysed(i)
+            spectral = total_ref[m] + part
+            degree = lax.axis_index("wave") * m_dev + m + lax.broadcasted_iota(jnp.int32, (1, degrees), 1)
+            growth = (degree * (degree + 1)).astype(jnp.float32)
+            scaled_growth = growth / (degrees * (degrees - 1))
+            square = scaled_growth * scaled_growth
+            for f in range(fields):
+                if f != 1:
+                    inverse = 1.0 / (1.0 + diff_ref[f] * square)
+                    for c in range(parts):
+                        first = c * feats + f * lev_dev
+                        out_ref[f, :, i, c, :] = spectral[first : first + lev_dev] * inverse
+            modal = [spectral[c * feats + lev_dev : c * feats + 2 * lev_dev] for c in range(parts)]
+            rates = lax.dot_general(
+                rates_ref[...], growth, (((0,), (0,)), ((), ())), precision=lax.Precision.HIGHEST, preferred_element_type=jnp.float32
+            )
+            amplitude = halves(jnp.concatenate(modal, axis=0) / (1.0 + rates))
+            inverse = 1.0 / (1.0 + diff_ref[1] * square)
+            mine = dot3(own, amplitude, ((1,), (0,))) * inverse
+            for c in range(parts):
+                out_ref[1, :, i, c, :] = mine
+            hold_ref[late_block, i] = encode(dot3(other, amplitude, ((1,), (0,))) * inverse, back_octaves, back_top)
+
+    @pl.when(step == pl.num_programs(0) - 1)
+    def _():
+        swap(blocks - 1).start()
+        lax.fori_loop(0, chunks, lambda at, _: (wait_most(there_ref, here_ref, there_sems.at[0, at], at, count), 0)[1], 0)
+        lax.fori_loop(0, rows, lambda at, _: (wait_most(back_ref, home_ref, back_sems.at[0, at], at, count), 0)[1], 0)
+        lax.fori_loop(0, blocks, lambda at, _: (swap(at).wait(), 0)[1], 0)
+
+
+def whole_step(state, legendre, lat, diffusion, modes, rates, gain, b1, b2, b3, perm, synthesis, analysis, w1, w2, w3):
+    fields, lev_dev, m_dev, parts, degrees = state.shape
+    waves, slabs = lax.axis_size("wave"), lax.axis_size("level")
+    count, feats, mc = waves * slabs, fields * lev_dev, m_dev * parts
+    tile = legendre.shape[1] // (waves * chunks)
+    legendre = legendre.reshape(m_dev, waves, chunks, tile, degrees)
+    per_chunk = tile // slabs
+    rows = chunks * per_chunk
+    m_block = 4
+    blocks = m_dev // m_block
+    first_steps = chunks * blocks
+    last = first_steps - 1
+    grid_steps = first_steps + rows
+    there = (chunks, count, per_chunk * mc, feats)
+    back = (rows, count, mc, feats)
+    small = (modes, rates, gain, b1, b2, b3, perm)
+    large = (synthesis, analysis, w1, w2, w3)
+    swap = (blocks, m_block, lev_dev, degrees)
+    any_spec = pl.BlockSpec(memory_space=pl.ANY)
+    smem = pl.BlockSpec(memory_space=pltpu.SMEM)
+    bf16, f32 = jnp.bfloat16, jnp.float32
+    pair = lambda i: jnp.where(i < first_steps, i, jnp.maximum(i - grid_steps, 0))
+    return pl.pallas_call(
+        step_kernel,
+        grid=(grid_steps + first_steps,),
+        out_shape=(jax.ShapeDtypeStruct(state.shape, f32), jax.ShapeDtypeStruct(swap, bf16)),
+        in_specs=[
+            smem,
+            smem,
+            pl.BlockSpec((fields, lev_dev, m_block, parts, degrees), lambda i: (0, 0, jnp.minimum(i, last) % blocks, 0, 0)),
+            pl.BlockSpec((m_block, waves, None, tile, degrees), lambda i: (pair(i) % blocks, 0, pair(i) // blocks, 0, 0)),
+            *[whole_block(x) for x in small],
+            *[any_spec for _ in large],
+        ],
+        out_specs=(
+            pl.BlockSpec((fields, lev_dev, m_block, parts, degrees), lambda i: (0, 0, jnp.maximum(i - (grid_steps + first_steps - blocks), 0), 0, 0)),
+            any_spec,
+        ),
+        scratch_shapes=[
+            pltpu.VMEM((count * per_chunk * mc, feats), f32),
+            pltpu.VMEM(there, bf16),
+            pltpu.VMEM(there, bf16),
+            pltpu.VMEM(back, bf16),
+            pltpu.VMEM(back, bf16),
+            pltpu.VMEM((m_dev, parts * feats, degrees), f32),
+            pltpu.VMEM(swap, bf16),
+            pltpu.VMEM((slabs * feats, slabs * feats), f32),
+            pltpu.VMEM(gain.shape, f32),
+            pltpu.VMEM(b3.shape, f32),
+            *[pltpu.VMEM(x.shape, bf16) for x in large],
+            pltpu.SemaphoreType.DMA((2, chunks)),
+            pltpu.SemaphoreType.DMA((2, rows)),
+            pltpu.SemaphoreType.DMA((2, blocks)),
+            pltpu.SemaphoreType.DMA((len(large),)),
+        ],
+        compiler_params=remote_params(),
+    )(lat, diffusion, state, legendre, *small, *large)
+
+
+def merge_kernel(old_ref, got_ref, out_ref):
+    level = lax.axis_index("level")
+    got = jnp.swapaxes(decode(got_ref[0], back_octaves, back_top), 0, 1)
+    for f in range(out_ref.shape[0]):
+        if f != 1:
+            out_ref[f] = old_ref[f]
+    for c in range(2):
+        out_ref[1, :, :, c, :] = jnp.where(level == c, old_ref[1, :, :, c, :], got)
+
+
+def merge_step(state, got):
+    fields, lev_dev, m_dev, parts, degrees = state.shape
+    blocks, m_block = got.shape[:2]
+    block = pl.BlockSpec((fields, lev_dev, m_block, parts, degrees), lambda i: (0, 0, i, 0, 0))
+    return pl.pallas_call(
+        merge_kernel,
+        grid=(blocks,),
+        out_shape=jax.ShapeDtypeStruct(state.shape, jnp.float32),
+        in_specs=[block, pl.BlockSpec((1, m_block, lev_dev, degrees), lambda i: (i, 0, 0, 0))],
+        out_specs=block,
+    )(state, got)
+
+
+def fast_body(longitudes, state, legendre, lat_weight, modes, mode_rates, diffusion, norm_gain, w_first, b_first, w_second, b_second, w_third, b_third):
+    fields, lev_dev, m_dev, parts, degrees = state.shape
+    levels = modes.shape[0]
+    wave_count, level_count = lax.axis_size("wave"), lax.axis_size("level")
+    synthesis, analysis = fourier_tables(degrees, longitudes, wave_count, 1.0)
+    place = np.arange(fields * levels).reshape(fields, level_count, lev_dev).swapaxes(0, 1).reshape(-1)
+    perm = np.zeros((fields * levels, fields * levels), jnp.bfloat16)
+    perm[place, np.arange(fields * levels)] = 1.0
+    out, got = whole_step(
+        state,
+        legendre,
+        lat_weight,
+        diffusion,
+        modes,
+        mode_rates[None],
+        norm_gain[None],
+        b_first[None],
+        b_second[None],
+        b_third[None],
+        perm,
+        synthesis,
+        analysis,
+        w_first,
+        w_second,
+        w_third,
+    )
+    return merge_step(out, got)
+
+
 def solution(mesh):
+    wave_count, level_count = mesh.shape["wave"], mesh.shape["level"]
+
     def step(state, legendre, *rest):
         longitudes = 2 * legendre.shape[1]
+        fields, levels, waves, _, degrees = state.shape
+        fits = (
+            level_count == 2
+            and waves % (16 * wave_count) == 0
+            and fields * levels % (128 * level_count) == 0
+            and levels % (8 * level_count) == 0
+            and legendre.shape[1] % (8 * chunks * wave_count) == 0
+            and degrees % 128 == 0
+        )
         mapped = jax.shard_map(
-            functools.partial(body, longitudes),
+            functools.partial(fast_body if fits else general_body, longitudes),
             mesh=mesh,
             in_specs=(P(None, "level", "wave", None, None), P("wave", None, None), P("wave")) + (P(),) * 10,
             out_specs=P(None, "level", "wave", None, None),

time: 623 us -> 175 us (0.28); the launches traced: 613 us -> 175 us
  local copies, waits for them, and re-layouts: 154 us -> 0 us
  blocking collectives: 150 us -> 0 us
  Pallas kernels: 43.4 us -> 175 us
  matrix products: 109 us -> 0 us
  other arithmetic: 89.5 us -> 0 us
  waiting for transfers between devices: 55.5 us -> 0 us
  starting transfers between devices: 11.3 us -> 0 us
    unnamed x1 -> x0, blocking collectives: 150 us -> none
    pallas_call x1 -> x2, Pallas kernels: 43.4 us -> 175 us  [the longest x1 169 us: whole_step(): pl.pallas_call(step_kernel, grid=(grid_steps + first_steps,), out_shape=(...]
    dot_general x6 -> x0, matrix products: 109 us -> none  [the longest x1 51.2 us: body(): grid = jnp.einsum('wvamcfl,wmco->aovfl', band, inverse_tab, precision=high)]
    all_to_all x2 -> x0, waiting for transfers between devices: 55.5 us -> none  [the longest x1 55.5 us: body(): band = lax.all_to_all(band, axes, split_axis=0, concat_axis=0, tiled=True)]
    reshape x7 -> x0, local copies, waits for them, and re-layouts: 52.2 us -> none  [the longest x1 20.1 us: body(): others.reshape(wave_count, m_dev, parts, lat_own, level_count, (fields -...]
    mul x6 -> x0, other arithmetic: 39.9 us -> none  [the longest x2 15.7 us: body(): basis = legendre * kept_mask[:, None, :]]
    slice x8 -> x0, local copies, waits for them, and re-layouts: 32.7 us -> none  [the longest x2 15.6 us: body(): others = jnp.concatenate([wave[..., :1, :], wave[..., 2:, :]], axis=-2)]
    unnamed x31 -> x0, local copies, waits for them, and re-layouts: 31.8 us -> none
  transfers between devices with their start and end apart: 2 -> 0, of which waited for: 1 -> 0; matrix products, arithmetic and copies ran while one was open for 4% -> 0% of each run, Pallas kernels for 0% -> 0%
where the time goes in v1:
time: 175 us
  Pallas kernels  175 us (100%)
    pallas_call x1, Pallas kernels, whole_step(): pl.pallas_call(step_kernel, grid=(grid_steps + first_steps,), out_shape=(...  169 us
    pallas_call x1, Pallas kernels, merge_step(): pl.pallas_call(merge_kernel, grid=(blocks,), out_shape=jax.ShapeDtypeStru...  5.26 us

profile of v1, /device:TPU:0, one launch (start us, length us, event | category | flops | bytes accessed | tf_op | source)
XLA Modules:
  0.0 174.6 jit_solution(8032586251117673544)
XLA Ops:
  0.0 169.4 %shard_map.154 = (f32[4,32,16,2,256]{4,3,2,1,0:T(2,128)}, bf16[4,4,32,256]{3,2,1,0:T(8,128)(2,1)}) custom-call(f32[24]{0:T(128)} %lat_ref.1, f32[4]{0:T(128)} %diff_ref.1, f32[4,32,16,2,256]{4,3,2,1,0:T(2,128)} %state_ref.1, f32[16,16,3,8,256]{4,3,2,1,0:T(8,128)} %bitcast.6, f32[64,64]{1,0:T(8,128)} %modes_ref.1, f32[1,64]{1,0:T(1,128)} %bitcast.11, ...), custom_call_target="tpu_custom_call" | custom-call | tf_op jit(solution)/shard_map/pallas_call | solution.py:525
  169.4 5.3 %shard_map.155 = f32[4,32,16,2,256]{4,3,2,1,0:T(2,128)} custom-call(f32[4,32,16,2,256]{4,3,2,1,0:T(2,128)} %get-tuple-element.7.old_ref, bf16[4,4,32,256]{3,2,1,0:T(8,128)(2,1)} %get-tuple-element.8.got_ref), custom_call_target="tpu_custom_call" | custom-call | tf_op jit(solution)/shard_map/pallas_call | solution.py:576

commit v2 on v1

--- a/solution.py
+++ b/solution.py
@@ -194,7 +194,7 @@
     per_wave = waves // wave_count
     synthesis, analysis = [], []
     for parity in range(2):
-        order = np.arange(waves).reshape(wave_count, per_wave // 2, 2)[:, :, parity]
+        order = np.arange(waves).reshape(wave_count * 2, per_wave // 4, 2)[:, :, parity]
         turns = order[:, :, None] * np.arange(half)[None, None, :] % longitudes
         angles = 2.0 * np.pi / longitudes * turns
         pair = np.stack([np.cos(angles), -np.sin(angles)], axis=1)
@@ -220,8 +220,8 @@
 
 
 def row_of(m, part, m_dev):
-    half = m_dev // 2
-    return (m % 2) * m_dev + part * half + m // 2
+    half, quarter = m_dev // 2, m_dev // 4
+    return m // half * m_dev + m % 2 * half + part * quarter + m % half // 2
 
 
 send_octaves, send_top = 32, 5
@@ -251,13 +251,28 @@
     return jnp.where(code < 0.0, -value, value)
 
 
+lanes = 128
+
+
+def by_lanes(x):
+    fields, lev, waves, parts, degrees = x.shape
+    x = x.reshape(fields, lev, waves, parts, degrees // lanes, lanes).transpose(0, 1, 2, 4, 3, 5)
+    return x.reshape(fields * lev, waves * (degrees // lanes) * parts, lanes)
+
+
+def from_lanes(x, dims):
+    fields, lev, waves, parts, degrees = dims
+    x = x.reshape(fields, lev, waves, degrees // lanes, parts, lanes).transpose(0, 1, 2, 4, 3, 5)
+    return x.reshape(dims)
+
+
 def own_place():
     slabs = lax.axis_size("level")
     count = lax.axis_size("wave") * slabs
     return lax.axis_index("wave") * slabs + lax.axis_index("level"), count, slabs
 
 
-def start_wave(src, dst, sems, at):
+def start_wave(src, dst, sems, at, sem):
     me, count, slabs = own_place()
     half = count // 2
     side = me // half
@@ -265,10 +280,10 @@
     def to(base, first):
         peer = base * half + lax.rem(me + first, half)
         pltpu.make_async_remote_copy(
-            src_ref=src.at[at, peer],
-            dst_ref=dst.at[at, me],
-            send_sem=sems.at[0, at],
-            recv_sem=sems.at[1, at],
+            src_ref=src.at[at(peer)],
+            dst_ref=dst.at[at(me)],
+            send_sem=sems.at[0, sem],
+            recv_sem=sems.at[1, sem],
             device_id=(peer // slabs, lax.rem(peer, slabs)),
             device_id_type=pl.DeviceIdType.MESH,
         ).start()
@@ -279,8 +294,8 @@
 
 
 def wait_most(src, dst, sem, at, count):
-    most = pl.ds(0, count - 1)
-    pltpu.make_async_copy(src.at[at, most], dst.at[at, most], sem).wait()
+    most = at(pl.ds(0, count - 1))
+    pltpu.make_async_copy(src.at[most], dst.at[most], sem).wait()
 
 
 def whole_block(x):
@@ -302,9 +317,23 @@
     band_ref, there_ref, here_ref, back_ref, home_ref, total_ref, hold_ref, modal_ref, gain_own, b3_own, syn_ref, ana_ref, w1_ref, w2_ref, w3_ref,
     there_sems, back_sems, swap_sems, load_sems,
 ):
-    fields, lev_dev, m_block, parts, degrees = state_ref.shape
+    m_block, _, _, degrees = leg_ref.shape
+    tiles = degrees // lanes
+    fields, lev_dev = diff_ref.shape[0], hold_ref.shape[2]
+    per_m = state_ref.shape[1] // m_block
+    parts = per_m // tiles
     rows = back_ref.shape[0]
     step = pl.program_id(0)
+    state_rows = state_ref.reshape(state_ref.shape[0] * state_ref.shape[1], lanes)
+    out_rows = out_ref.reshape(out_ref.shape[0] * out_ref.shape[1], lanes)
+
+    def place_of(f, i, c, t):
+        return pl.ds(f * lev_dev * m_block * per_m + i * per_m + t * parts + c, lev_dev, stride=m_block * per_m)
+
+    def put(f, i, c, value):
+        for t in range(tiles):
+            out_rows[place_of(f, i, c, t), :] = value[:, t * lanes : (t + 1) * lanes]
+
     first_steps = (pl.num_programs(0) - rows) // 2
     blocks = first_steps // chunks
     grid_steps = first_steps + rows
@@ -322,16 +351,30 @@
         for i, (src, dst) in enumerate(((syn_hbm, syn_ref), (ana_hbm, ana_ref), (w1_hbm, w1_ref), (w2_hbm, w2_ref), (w3_hbm, w3_ref)))
     ]
 
-    @pl.when(step == 0)
+    @pl.when(step == blocks)
     def _():
         for load in loads:
             load.start()
 
-    @pl.when((step > 0) & (step <= first_steps) & (lax.rem(step, blocks) == 0))
-    def _():
-        start_wave(there_ref, here_ref, there_sems, step // blocks - 1)
-
-    @pl.when(step == blocks)
+    per_half = blocks // 2
+    part_of = lambda h: pl.ds(pl.multiple_of(h * half, half), half)
+
+    def there_at(sem):
+        return lambda peer: (sem // 2, peer, slice(None), part_of(lax.rem(sem, 2)))
+
+    def row_at(row):
+        return lambda peer: (row, peer)
+
+    def tail_at(sem):
+        place = sem - (rows - per_chunk)
+        return lambda peer: (rows - per_chunk + lax.rem(place, per_chunk), peer, part_of(place // per_chunk))
+
+    @pl.when((step > 0) & (step <= first_steps) & (lax.rem(step, per_half) == 0))
+    def _():
+        sem = step // per_half - 1
+        start_wave(there_ref, here_ref, there_sems, there_at(sem), sem)
+
+    @pl.when(step == first_steps - 1)
     def _():
         for load in loads:
             load.wait()
@@ -356,29 +399,42 @@
             m = block * m_block + i
             basis = leg_ref[i].reshape(-1, degrees)
             basis = halves(kept(basis, lax.axis_index("wave") * m_dev + m))
-            coeffs = [state_ref[:, :, i, c, :].reshape(feats, degrees) for c in range(parts)]
+            coeffs = []
+            for c in range(parts):
+                pieces = [state_rows[pl.ds(i * per_m + t * parts + c, feats, stride=m_block * per_m), :] for t in range(tiles)]
+                coeffs.append(jnp.concatenate(pieces, axis=1))
             coeffs = halves(jnp.concatenate(coeffs, axis=0))
             band = dot3(basis, coeffs, ((1,), (1,)))
             for c in range(parts):
                 at = pl.ds(row_of(m, c, m_dev), band.shape[0], stride=mc)
                 band_ref[at, :] = band[:, c * feats : (c + 1) * feats]
 
-        @pl.when(block == blocks - 1)
+        @pl.when(lax.rem(block, per_half) == per_half - 1)
         def _():
-            size = per_chunk * mc
             many = 4
+            part = part_of(block // per_half)
+            rows_of = band_ref.reshape(count, per_chunk, mc, feats)
 
             def one(k, _):
-                part = band_ref[pl.ds(pl.multiple_of(k * many * size, 8), many * size), :]
-                there_ref[group, pl.ds(k * many, many)] = encode(part, send_octaves, send_top).reshape(many, size, feats)
+                at = pl.ds(k * many, many)
+                there_ref[group, at, :, part] = encode(rows_of[at, :, part, :], send_octaves, send_top)
                 return 0
 
             lax.fori_loop(0, count // many, one, 0)
-            here_ref[group, me] = there_ref[group, me]
-
-    @pl.when((step > first_steps) & (step <= grid_steps))
-    def _():
-        start_wave(back_ref, home_ref, back_sems, step - first_steps - 1)
+            here_ref[group, me, :, part] = there_ref[group, me, :, part]
+
+    @pl.when((step > first_steps) & (step <= grid_steps - per_chunk))
+    def _():
+        row = step - first_steps - 1
+        start_wave(back_ref, home_ref, back_sems, row_at(row), row)
+
+    @pl.when(step == grid_steps)
+    def _():
+        def tail(sem, _):
+            start_wave(back_ref, home_ref, back_sems, tail_at(sem), sem)
+            return 0
+
+        lax.fori_loop(rows - per_chunk, rows + per_chunk, tail, 0)
 
     @pl.when((step >= first_steps) & (step < grid_steps))
     def _():
@@ -387,13 +443,14 @@
 
         @pl.when(place == 0)
         def _():
-            wait_most(there_ref, here_ref, there_sems.at[1, group], group, count)
+            for h in range(2):
+                sem = 2 * group + h
+                wait_most(there_ref, here_ref, there_sems.at[1, sem], there_at(sem), count)
 
         signs = []
+        decoded = decode(here_ref[group, :, place], send_octaves, send_top).reshape(waves, slabs, 2, 2, half // 2, feats)
         for parity in range(2):
-            at = pl.ds(pl.multiple_of(place * mc + parity * half, half), half)
-            band = decode(here_ref[group, :, at, :], send_octaves, send_top).reshape(waves, slabs, half, feats)
-            band = [band[:, v].reshape(waves * half, feats) for v in range(slabs)]
+            band = [decoded[:, v, :, parity].reshape(waves * half, feats) for v in range(slabs)]
             band = halves(jnp.concatenate(band, axis=1))
             signs.append(dot3((syn_ref[parity, 0], syn_ref[parity, 1]), band, ((1,), (0,))))
         weight = lat_ref[group * (slabs * per_chunk) + level * per_chunk + place]
@@ -408,31 +465,51 @@
             updated.append((grid + tendency.astype(jnp.float32)) * weight)
         folded = (updated[0] + updated[1], updated[0] - updated[1])
         modal = halves(modal_ref[...])
-        lane = lax.broadcasted_iota(jnp.int32, (waves, half // 2, feats), 2)
+        lane = lax.broadcasted_iota(jnp.int32, (waves * half, feats), 1)
+        line = lax.rem(lax.broadcasted_iota(jnp.int32, (waves * half, feats), 0), half // 2) // (half // 4)
         swapped = (lane >= lev_dev) & (lane < 2 * lev_dev)
+        sent = []
         for parity in range(2):
             wave = dot3((ana_ref[parity, 0], ana_ref[parity, 1]), halves(folded[parity]), ((1,), (0,)))
             wave = dot3(halves(wave), modal, ((1,), (0,)))
-            piece = lambda c, v: wave[:, v * feats : (v + 1) * feats].reshape(waves, 2, half // 2, feats)[:, c]
+            slab = [wave[:, v * feats : (v + 1) * feats] for v in range(slabs)]
+            turned = []
             for v in range(slabs):
-                both = [jnp.where(swapped, piece(v, c), piece(c, v)) for c in range(2)]
-                both = encode(jnp.concatenate(both, axis=1), back_octaves, back_top)
-                for w in range(waves):
-                    back_ref[row, w * slabs + v, parity * half : (parity + 1) * half, :] = both[w]
-
+                other = slab[1 - v].reshape(waves * 2, half // 2, feats)
+                other = pltpu.roll(other, half // 4, 1).reshape(waves * half, feats)
+                turned.append(jnp.where(swapped & (line == 1 - v), other, slab[v]).reshape(waves, 2, half // 2, feats))
+            sent.append(turned)
+        for v in range(slabs):
+            both = jnp.concatenate([sent[0][v], sent[1][v]], axis=2).reshape(waves, mc, feats)
+            both = encode(both, back_octaves, back_top)
+            for w in range(waves):
+                back_ref[row, w * slabs + v] = both[w]
         home_ref[row, me] = back_ref[row, me]
 
     late = step - grid_steps
     late_group, late_block = late // blocks, lax.rem(late, blocks)
 
-    @pl.when((step >= grid_steps) & (late_block == 0))
-    def _():
-        wave_ref = band_ref.reshape(count, per_chunk, mc, feats)
-
+    wave_ref = band_ref.reshape(count, per_chunk, mc, feats)
+
+    @pl.when((step >= grid_steps) & (late_group < chunks - 1) & (late_block == 0))
+    def _():
         def one(r, _):
             row = late_group * per_chunk + r
-            wait_most(back_ref, home_ref, back_sems.at[1, row], row, count)
+            wait_most(back_ref, home_ref, back_sems.at[1, row], row_at(row), count)
             wave_ref[:, r] = decode(home_ref[row], back_octaves, back_top)
+            return 0
+
+        lax.fori_loop(0, per_chunk, one, 0)
+
+    @pl.when((step >= grid_steps) & (late_group == chunks - 1) & (lax.rem(late_block, per_half) == 0))
+    def _():
+        h = late_block // per_half
+
+        def one(r, _):
+            row = rows - per_chunk + r
+            sem = row + h * per_chunk
+            wait_most(back_ref, home_ref, back_sems.at[1, sem], tail_at(sem), count)
+            wave_ref[:, r, part_of(h)] = decode(home_ref[row, :, part_of(h)], back_octaves, back_top)
             return 0
 
         lax.fori_loop(0, per_chunk, one, 0)
@@ -462,10 +539,6 @@
 
     @pl.when((step >= grid_steps) & (late_group == chunks - 1))
     def _():
-        @pl.when(late_block > 0)
-        def _():
-            swap(late_block - 1).start()
-
         own = halves(modes_ref[pl.ds(pl.multiple_of(level * lev_dev, 8), lev_dev), :])
         other = halves(modes_ref[pl.ds(pl.multiple_of((1 - level) * lev_dev, 8), lev_dev), :])
         for i in range(m_block):
@@ -480,7 +553,7 @@
                     inverse = 1.0 / (1.0 + diff_ref[f] * square)
                     for c in range(parts):
                         first = c * feats + f * lev_dev
-                        out_ref[f, :, i, c, :] = spectral[first : first + lev_dev] * inverse
+                        put(f, i, c, spectral[first : first + lev_dev] * inverse)
             modal = [spectral[c * feats + lev_dev : c * feats + 2 * lev_dev] for c in range(parts)]
             rates = lax.dot_general(
                 rates_ref[...], growth, (((0,), (0,)), ((), ())), precision=lax.Precision.HIGHEST, preferred_element_type=jnp.float32
@@ -489,14 +562,15 @@
             inverse = 1.0 / (1.0 + diff_ref[1] * square)
             mine = dot3(own, amplitude, ((1,), (0,))) * inverse
             for c in range(parts):
-                out_ref[1, :, i, c, :] = mine
+                put(1, i, c, mine)
             hold_ref[late_block, i] = encode(dot3(other, amplitude, ((1,), (0,))) * inverse, back_octaves, back_top)
+        swap(late_block).start()
 
     @pl.when(step == pl.num_programs(0) - 1)
     def _():
-        swap(blocks - 1).start()
-        lax.fori_loop(0, chunks, lambda at, _: (wait_most(there_ref, here_ref, there_sems.at[0, at], at, count), 0)[1], 0)
-        lax.fori_loop(0, rows, lambda at, _: (wait_most(back_ref, home_ref, back_sems.at[0, at], at, count), 0)[1], 0)
+        lax.fori_loop(0, 2 * chunks, lambda at, _: (wait_most(there_ref, here_ref, there_sems.at[0, at], there_at(at), count), 0)[1], 0)
+        lax.fori_loop(0, rows - per_chunk, lambda at, _: (wait_most(back_ref, home_ref, back_sems.at[0, at], row_at(at), count), 0)[1], 0)
+        lax.fori_loop(rows - per_chunk, rows + per_chunk, lambda at, _: (wait_most(back_ref, home_ref, back_sems.at[0, at], tail_at(at), count), 0)[1], 0)
         lax.fori_loop(0, blocks, lambda at, _: (swap(at).wait(), 0)[1], 0)
 
 
@@ -513,11 +587,13 @@
     first_steps = chunks * blocks
     last = first_steps - 1
     grid_steps = first_steps + rows
-    there = (chunks, count, per_chunk * mc, feats)
+    there = (chunks, count, per_chunk, mc, feats)
     back = (rows, count, mc, feats)
     small = (modes, rates, gain, b1, b2, b3, perm)
     large = (synthesis, analysis, w1, w2, w3)
     swap = (blocks, m_block, lev_dev, degrees)
+    lined = by_lanes(state)
+    line_block = (lined.shape[0], lined.shape[1] // blocks, lanes)
     any_spec = pl.BlockSpec(memory_space=pl.ANY)
     smem = pl.BlockSpec(memory_space=pltpu.SMEM)
     bf16, f32 = jnp.bfloat16, jnp.float32
@@ -525,17 +601,17 @@
     return pl.pallas_call(
         step_kernel,
         grid=(grid_steps + first_steps,),
-        out_shape=(jax.ShapeDtypeStruct(state.shape, f32), jax.ShapeDtypeStruct(swap, bf16)),
+        out_shape=(jax.ShapeDtypeStruct(lined.shape, f32), jax.ShapeDtypeStruct(swap, bf16)),
         in_specs=[
             smem,
             smem,
-            pl.BlockSpec((fields, lev_dev, m_block, parts, degrees), lambda i: (0, 0, jnp.minimum(i, last) % blocks, 0, 0)),
+            pl.BlockSpec(line_block, lambda i: (0, jnp.minimum(i, last) % blocks, 0)),
             pl.BlockSpec((m_block, waves, None, tile, degrees), lambda i: (pair(i) % blocks, 0, pair(i) // blocks, 0, 0)),
             *[whole_block(x) for x in small],
             *[any_spec for _ in large],
         ],
         out_specs=(
-            pl.BlockSpec((fields, lev_dev, m_block, parts, degrees), lambda i: (0, 0, jnp.maximum(i - (grid_steps + first_steps - blocks), 0), 0, 0)),
+            pl.BlockSpec(line_block, lambda i: (0, jnp.maximum(i - (grid_steps + first_steps - blocks), 0), 0)),
             any_spec,
         ),
         scratch_shapes=[
@@ -550,36 +626,42 @@
             pltpu.VMEM(gain.shape, f32),
             pltpu.VMEM(b3.shape, f32),
             *[pltpu.VMEM(x.shape, bf16) for x in large],
-            pltpu.SemaphoreType.DMA((2, chunks)),
-            pltpu.SemaphoreType.DMA((2, rows)),
+            pltpu.SemaphoreType.DMA((2, 2 * chunks)),
+            pltpu.SemaphoreType.DMA((2, rows + per_chunk)),
             pltpu.SemaphoreType.DMA((2, blocks)),
             pltpu.SemaphoreType.DMA((len(large),)),
         ],
         compiler_params=remote_params(),
-    )(lat, diffusion, state, legendre, *small, *large)
-
-
-def merge_kernel(old_ref, got_ref, out_ref):
-    level = lax.axis_index("level")
-    got = jnp.swapaxes(decode(got_ref[0], back_octaves, back_top), 0, 1)
-    for f in range(out_ref.shape[0]):
-        if f != 1:
-            out_ref[f] = old_ref[f]
-    for c in range(2):
-        out_ref[1, :, :, c, :] = jnp.where(level == c, old_ref[1, :, :, c, :], got)
-
-
-def merge_step(state, got):
-    fields, lev_dev, m_dev, parts, degrees = state.shape
-    blocks, m_block = got.shape[:2]
-    block = pl.BlockSpec((fields, lev_dev, m_block, parts, degrees), lambda i: (0, 0, i, 0, 0))
+    )(lat, diffusion, lined, legendre, *small, *large)
+
+
+def merge_kernel(parts, old_ref, got_ref, out_ref):
+    lev_dev, per_lev, _ = out_ref.shape
+    blocks, m_block, _, degrees = got_ref.shape
+    tiles = degrees // lanes
+    other = 1 - lax.axis_index("level")
+    out_ref[...] = old_ref[...]
+
+    @pl.when(pl.program_id(0) == 1)
+    def _():
+        out_rows = out_ref.reshape(lev_dev * per_lev, lanes)
+        for b in range(blocks):
+            for i in range(m_block):
+                value = decode(got_ref[b, i], back_octaves, back_top)
+                for t in range(tiles):
+                    at = ((b * m_block + i) * tiles + t) * parts + other
+                    out_rows[pl.ds(at, lev_dev, stride=per_lev), :] = value[:, t * lanes : (t + 1) * lanes]
+
+
+def merge_step(fields, parts, lined, got):
+    block = pl.BlockSpec((lined.shape[0] // fields, *lined.shape[1:]), lambda i: (i, 0, 0))
     return pl.pallas_call(
-        merge_kernel,
-        grid=(blocks,),
-        out_shape=jax.ShapeDtypeStruct(state.shape, jnp.float32),
-        in_specs=[block, pl.BlockSpec((1, m_block, lev_dev, degrees), lambda i: (i, 0, 0, 0))],
+        functools.partial(merge_kernel, parts),
+        grid=(fields,),
+        out_shape=jax.ShapeDtypeStruct(lined.shape, jnp.float32),
+        in_specs=[block, whole_block(got)],
         out_specs=block,
-    )(state, got)
+    )(lined, got)
 
 
 def fast_body(longitudes, state, legendre, lat_weight, modes, mode_rates, diffusion, norm_gain, w_first, b_first, w_second, b_second, w_third, b_third):
@@ -608,7 +690,7 @@
         w_second,
         w_third,
     )
-    return merge_step(out, got)
+    return from_lanes(merge_step(fields, parts, out, got), state.shape)
 
 
 def solution(mesh):

time: 175 us -> 170 us (0.971)
  Pallas kernels: 175 us -> 169 us
    pallas_call x1, Pallas kernels: 169 us -> 164 us  [whole_step(): pl.pallas_call(step_kernel, grid=(grid_steps + first_steps,), out_shape=(...]
where the time goes in v2:
time: 170 us; the launch traced here: 169 us
  Pallas kernels  169 us (99%)
    pallas_call x1, Pallas kernels, whole_step(): pl.pallas_call(step_kernel, grid=(grid_steps + first_steps,), out_shape=(...  164 us
    pallas_call x1, Pallas kernels, merge_step(): pl.pallas_call(functools.partial(merge_kernel, parts), grid=(fields,), ou...  5.1 us

profile of v2, /device:TPU:0, one launch (start us, length us, event | category | flops | bytes accessed | tf_op | source)
XLA Modules:
  0.0 169.3 jit_solution(17301917384415676228)
XLA Ops:
  0.0 164.2 %shard_map.154 = (f32[128,64,128]{2,1,0:T(8,128)}, bf16[4,4,32,256]{3,2,1,0:T(8,128)(2,1)}) custom-call(f32[24]{0:T(128)} %lat_ref.1, f32[4]{0:T(128)} %diff_ref.1, f32[128,64,128]{2,1,0:T(8,128)} %bitcast.17, f32[16,16,3,8,256]{4,3,2,1,0:T(8,128)} %bitcast.16, f32[64,64]{1,0:T(8,128)} %modes_ref.1, f32[1,64]{1,0:T(1,128)} %bitcast.22, f32[1,256]{1,0:T(1,128)} %bitcast.20, ...), custom_call_target="tpu_custom_call" | custom-call | tf_op jit(solution)/shard_map/pallas_call | solution.py:601
  164.2 5.1 %shard_map.155 = f32[128,64,128]{2,1,0:T(8,128)} custom-call(f32[128,64,128]{2,1,0:T(8,128)} %get-tuple-element.7.old_ref, bf16[4,4,32,256]{3,2,1,0:T(8,128)(2,1)} %get-tuple-element.8.got_ref), custom_call_target="tpu_custom_call" | custom-call | tf_op jit(solution)/shard_map/pallas_call | solution.py:658

commit v3 on v2

--- a/solution.py
+++ b/solution.py
@@ -360,7 +360,7 @@
     part_of = lambda h: pl.ds(pl.multiple_of(h * half, half), half)
 
     def there_at(sem):
-        return lambda peer: (sem // 2, peer, slice(None), part_of(lax.rem(sem, 2)))
+        return lambda peer: (sem // 2, lax.rem(sem, 2), peer)
 
     def row_at(row):
         return lambda peer: (row, peer)
@@ -412,16 +412,17 @@
         @pl.when(lax.rem(block, per_half) == per_half - 1)
         def _():
             many = 4
-            part = part_of(block // per_half)
+            h = block // per_half
+            part = part_of(h)
             rows_of = band_ref.reshape(count, per_chunk, mc, feats)
 
             def one(k, _):
                 at = pl.ds(k * many, many)
-                there_ref[group, at, :, part] = encode(rows_of[at, :, part, :], send_octaves, send_top)
+                there_ref[group, h, at] = encode(rows_of[at, :, part, :], send_octaves, send_top)
                 return 0
 
             lax.fori_loop(0, count // many, one, 0)
-            here_ref[group, me, :, part] = there_ref[group, me, :, part]
+            here_ref[group, h, me] = there_ref[group, h, me]
 
     @pl.when((step > first_steps) & (step <= grid_steps - per_chunk))
     def _():
@@ -448,9 +449,9 @@
                 wait_most(there_ref, here_ref, there_sems.at[1, sem], there_at(sem), count)
 
         signs = []
-        decoded = decode(here_ref[group, :, place], send_octaves, send_top).reshape(waves, slabs, 2, 2, half // 2, feats)
+        decoded = [decode(here_ref[group, h, :, place], send_octaves, send_top).reshape(waves, slabs, 2, half // 2, feats) for h in range(2)]
         for parity in range(2):
-            band = [decoded[:, v, :, parity].reshape(waves * half, feats) for v in range(slabs)]
+            band = [jnp.concatenate([d[:, v, parity] for d in decoded], axis=1).reshape(waves * half, feats) for v in range(slabs)]
             band = halves(jnp.concatenate(band, axis=1))
             signs.append(dot3((syn_ref[parity, 0], syn_ref[parity, 1]), band, ((1,), (0,))))
         weight = lat_ref[group * (slabs * per_chunk) + level * per_chunk + place]
@@ -587,7 +588,7 @@
     first_steps = chunks * blocks
     last = first_steps - 1
     grid_steps = first_steps + rows
-    there = (chunks, count, per_chunk, mc, feats)
+    there = (chunks, 2, count, per_chunk, mc // 2, feats)
     back = (rows, count, mc, feats)
     small = (modes, rates, gain, b1, b2, b3, perm)
     large = (synthesis, analysis, w1, w2, w3)
@@ -636,28 +637,29 @@
 
 
 def merge_kernel(parts, old_ref, got_ref, out_ref):
-    lev_dev, per_lev, _ = out_ref.shape
-    blocks, m_block, _, degrees = got_ref.shape
+    per_block, per_lev, _ = out_ref.shape
+    blocks, m_block, lev_dev, degrees = got_ref.shape
     tiles = degrees // lanes
     other = 1 - lax.axis_index("level")
     out_ref[...] = old_ref[...]
 
-    @pl.when(pl.program_id(0) == 1)
-    def _():
-        out_rows = out_ref.reshape(lev_dev * per_lev, lanes)
+    @pl.when(pl.program_id(0) == 0)
+    def _():
+        out_rows = out_ref.reshape(per_block * per_lev, lanes)
         for b in range(blocks):
             for i in range(m_block):
                 value = decode(got_ref[b, i], back_octaves, back_top)
                 for t in range(tiles):
-                    at = ((b * m_block + i) * tiles + t) * parts + other
+                    at = lev_dev * per_lev + ((b * m_block + i) * tiles + t) * parts + other
                     out_rows[pl.ds(at, lev_dev, stride=per_lev), :] = value[:, t * lanes : (t + 1) * lanes]
 
 
 def merge_step(fields, parts, lined, got):
-    block = pl.BlockSpec((lined.shape[0] // fields, *lined.shape[1:]), lambda i: (i, 0, 0))
+    blocks = fields // 2 if fields % 2 == 0 else 1
+    block = pl.BlockSpec((lined.shape[0] // blocks, *lined.shape[1:]), lambda i: (i, 0, 0))
     return pl.pallas_call(
         functools.partial(merge_kernel, parts),
-        grid=(fields,),
+        grid=(blocks,),
         out_shape=jax.ShapeDtypeStruct(lined.shape, jnp.float32),
         in_specs=[block, whole_block(got)],
         out_specs=block,

time: 170 us -> 169 us (level)
  no operation moved by 1% of the time
where the time goes in v3:
time: 169 us; the launch traced here: 168 us
  Pallas kernels  168 us (99%)
    pallas_call x1, Pallas kernels, whole_step(): pl.pallas_call(step_kernel, grid=(grid_steps + first_steps,), out_shape=(...  164 us
    pallas_call x1, Pallas kernels, merge_step(): pl.pallas_call(functools.partial(merge_kernel, parts), grid=(blocks,), ou...  4.41 us

profile of v3, /device:TPU:0, one launch (start us, length us, event | category | flops | bytes accessed | tf_op | source)
XLA Modules:
  0.0 168.4 jit_solution(16609468571454433761)
XLA Ops:
  0.0 164.0 %shard_map.154 = (f32[128,64,128]{2,1,0:T(8,128)}, bf16[4,4,32,256]{3,2,1,0:T(8,128)(2,1)}) custom-call(f32[24]{0:T(128)} %lat_ref.1, f32[4]{0:T(128)} %diff_ref.1, f32[128,64,128]{2,1,0:T(8,128)} %bitcast.17, f32[16,16,3,8,256]{4,3,2,1,0:T(8,128)} %bitcast.16, f32[64,64]{1,0:T(8,128)} %modes_ref.1, f32[1,64]{1,0:T(1,128)} %bitcast.22, f32[1,256]{1,0:T(1,128)} %bitcast.20, ...), custom_call_target="tpu_custom_call" | custom-call | tf_op jit(solution)/shard_map/pallas_call | solution.py:602
  164.0 4.4 %shard_map.155 = f32[128,64,128]{2,1,0:T(8,128)} custom-call(f32[128,64,128]{2,1,0:T(8,128)} %get-tuple-element.7.old_ref, bf16[4,4,32,256]{3,2,1,0:T(8,128)(2,1)} %get-tuple-element.8.got_ref), custom_call_target="tpu_custom_call" | custom-call | tf_op jit(solution)/shard_map/pallas_call | solution.py:660
